TPU v7x, 256 devices: a 2x2x32 block of a 4x8x32 slice. The times are simulated.
256 devices in a mesh: band: 4 (over y, x), row: 64 (over z, core).
Axes of the slice: x: 2, y: 2, z: 32, core: 2. Of those that a mesh axis runs over, the one named last changes fastest.
The devices are a block of a 4x8x32 slice.
Arguments:
- shot_traces: bfloat16 [131072, 4096], P(('band', 'row')), parts along dimension 0, may hold values from -6 to 6
- source_cell: int32 [131072], P(('band', 'row')), parts along dimension 0, may hold values from 0 to 127
- receiver_cell: int32 [131072], P(('band', 'row')), parts along dimension 0, may hold values from 0 to 127
- band_order: int32 [512], P('band'), parts along dimension 0, may hold values from 0 to 127, each once
Outputs:
- next_grid: float32 [512, 2, 128, 128], P(('band', 'row')), parts along dimension 0
There are 4 independent parts, one for each index of `band`. A program takes and returns all parts, laid end to end along the dimension named above; each array names one. Nothing has to cross between parts.
Inputs may be any that keep to these rules, and one draw needn't show every extreme that they name: `band_order`: a permutation of 0 to 127.
All inputs are finite; a program needn't handle non-finite values.
Results may differ from a plain program's by a relative error of at most 0.0037.
Values may be sent and summed in bfloat16 or wider, within the bound.
A program may use at most 64 MiB of HBM per device.

v0:
```python
import math

import jax
import jax.numpy as jnp
from jax import lax
from jax.sharding import PartitionSpec as P

FLO = 64
SC = 128
RC = 128


def local(shot_traces, source_cell, receiver_cell, band_order):
    samples_count = shot_traces.shape[1]
    band_size = band_order.shape[0]
    local_traces = shot_traces.shape[0]
    bins = FLO + band_order
    samples = jnp.arange(samples_count, dtype=jnp.int32)
    phase = samples[:, None] * bins[None, :] % samples_count
    angle = 2.0 * math.pi * phase.astype(jnp.float32) / samples_count
    scale = 1.0 / math.sqrt(samples_count)
    table = jnp.concatenate([jnp.cos(angle) * scale, -jnp.sin(angle) * scale], axis=1).astype(
        jnp.bfloat16
    )
    spectra = jnp.dot(shot_traces, table, preferred_element_type=jnp.float32).astype(jnp.bfloat16)
    spectra = spectra.reshape(local_traces, 2, band_size)
    source_range = jnp.arange(SC, dtype=jnp.float32)
    receiver_range = jnp.arange(RC, dtype=jnp.float32)
    cells = jnp.stack([source_cell, receiver_cell], axis=1).astype(jnp.bfloat16)
    cells = jnp.broadcast_to(cells[:, :, None], (local_traces, 2, band_size))
    packed = jnp.concatenate([spectra, cells], axis=1)
    moved = lax.all_to_all(packed, "row", split_axis=2, concat_axis=0, tiled=True)
    received = moved[:, 0:2, :]
    source_value = moved[:, 2, 0].astype(jnp.float32)
    receiver_value = moved[:, 3, 0].astype(jnp.float32)
    source_hot = (source_value[:, None] == source_range[None, :]).astype(jnp.bfloat16)
    receiver_hot = (receiver_value[:, None] == receiver_range[None, :]).astype(jnp.bfloat16)
    counts = jnp.einsum("ts,tr->sr", source_hot, receiver_hot, preferred_element_type=jnp.float32)
    weighted = received[:, :, :, None] * receiver_hot[:, None, None, :]
    stack = jnp.einsum("ts,tcfr->fcsr", source_hot, weighted, preferred_element_type=jnp.float32)
    next_grid = stack / jnp.maximum(counts, 1.0)[None, None, :, :]
    return next_grid


def solution(mesh):
    placed = (P(("band", "row"), None), P(("band", "row")), P(("band", "row")), P("band"))
    return jax.shard_map(
        local,
        mesh=mesh,
        in_specs=placed,
        out_specs=P(("band", "row"), None, None, None),
        check_vma=False,
    )
```

profile of v0, /device:TPU:37, one launch (start us, length us, event | category | flops | bytes accessed | tf_op | source)
XLA Modules:
  0.0 156.7 jit_solution(13117734031525655496)
XLA Ops:
  0.0 0.7 broadcast_add_fusion
  0.7 0.7 convert.18
  1.4 0.7 convert.19
  2.0 8.6 %multiply_convert_fusion.1 = (bf16[4096,128]{1,0:T(8,128)(2,1)S(1)}, bf16[4096,128]{1,0:T(8,128)(2,1)S(1)}) fusion(s32[128]{0:T(128)S(1)} %broadcast_add_fusion), kind=kLoop, calls=%fused_computation.24 | loop fusion | flops 9961472 | bytes 2097664 | tf_op jit(solution)/shard_map/convert.6
  10.7 3.5 %fusion.23 = bf16[256,512]{1,0:T(8,128)(2,1)S(1)} fusion(bf16[512,4096]{1,0:T(8,128)(2,1)} %param.4, bf16[4096,128]{1,0:T(8,128)(2,1)S(1)} %get-tuple-element.8, bf16[4096,128]{1,0:T(8,128)(2,1)S(1)} %get-tuple-element.7), kind=kOutput, calls=%fused_computation.28 | convolution fusion | flops 1078067200 | bytes 6553600 | tf_op jit(solution)/shard_map/dot_general | solution.py:25
  14.2 0.3 copy.10
  14.5 0.1 broadcast_in_dim.2
  14.6 0.5 pad_maximum_fusion
  15.2 98.1 %all_to_all.18 = bf16[512,4,128]{0,1,2:T(4,128)(2,1)S(1)} all-to-all(bf16[512,4,128]{0,1,2:T(4,128)(2,1)S(1)} %pad_maximum_fusion), channel_id=1, replica_groups=mesh['band'=4,'row'=64] {'row'}, dimensions={2} | all-to-all | bytes 1048576 | tf_op jit(solution)/shard_map/all_to_all | solution.py:32
  113.3 0.2 copy.16
  113.4 0.4 all_to_all.16
  113.8 0.0 copy-start
  113.8 0.2 slice_convert_fusion.1
  114.0 2.2 %iota_compare_fusion.8 = pred[32768,128]{0,1:T(32,128)(4,1)S(1)} fusion(f32[32768]{0:T(1024)S(1)} %bitcast.37), kind=kLoop, calls=%fused_computation.6.clone.clone.clone.clone.2 | loop fusion | flops 4194304 | bytes 4325376 | tf_op jit(solution)/shard_map/ts,tr->sr/dot_general | solution.py:38
  116.2 4.9 %fusion.6 = bf16[32768,128]{0,1:T(8,128)(2,1)} fusion(f32[32768]{0:T(1024)S(1)} %bitcast.38), kind=kLoop, calls=%fused_computation.8 | loop fusion | flops 8388608 | bytes 8519680 | tf_op jit(solution)/shard_map/convert_element_type | solution.py:37
  121.1 0.0 copy-done
  121.1 14.4 %fusion.50 = pred[32768,128,1,1]{1,0,3,2:T(32,128)(4,1)} fusion(f32[32768]{0:T(1024)S(1)} %bitcast.39), kind=kLoop, calls=%fused_computation.4.clone.clone.clone.clone.clone.clone.2 | loop fusion | flops 4194304 | bytes 4325376 | tf_op jit(solution)/shard_map/ts,tcfr->fcsr/dot_general | solution.py:40
  135.5 0.0 slice-start
  135.5 7.1 %fusion.36 = f32[128,128]{1,0:T(8,128)S(1)} fusion(f32[32768]{0:T(1024)S(1)} %bitcast.40, pred[32768,128]{0,1:T(32,128)(4,1)S(1)} %iota_compare_fusion.8), kind=kOutput, calls=%fused_computation.31 | convolution fusion | flops 1082146816 | bytes 4390912 | tf_op jit(solution)/shard_map/ts,tr->sr/dot_general | solution.py:38
  142.7 0.1 copy.12
  142.8 0.0 slice-done
  142.8 13.1 %fusion.31 = f32[2,2,128,128]{2,3,0,1:T(8,128)S(1)} fusion(bf16[32768,128]{0,1:T(8,128)(2,1)} %fusion.6, bf16[32768,2,2]{0,2,1:T(2,128)(2,1)S(1)} %slice-done, f32[128,128]{0,1:T(8,128)S(1)} %copy.12, pred[32768,128,1,1]{1,0,3,2:T(32,128)(4,1)} %fusion.50), kind=kOutput, calls=%fused_computation.30 | convolution fusion | flops 4311810048 | bytes 13172736 | tf_op jit(solution)/shard_map/ts,tcfr->fcsr/dot_general | solution.py:40
  155.9 0.8 copy.13
  (3 shorter events, 0.0 us)
Async XLA Ops:
  113.8 7.3 %copy-start = (bf16[32768,4,2]{0,2,1:T(2,128)(2,1)}, bf16[32768,4,2]{0,2,1:T(2,128)(2,1)S(1)}, u32[]{:S(2)}) copy-start(bf16[32768,4,2]{0,2,1:T(2,128)(2,1)S(1)} %all_to_all.16) | copy-start | bytes 1572868
  135.5 7.2 %slice-start = ((bf16[32768,4,2]{0,2,1:T(2,128)(2,1)}), bf16[32768,2,2]{0,2,1:T(2,128)(2,1)S(1)}, s32[]{:S(2)}) async-start(bf16[32768,4,2]{0,2,1:T(2,128)(2,1)} %copy-done), calls=%async_computation.1 | async-start | bytes 524288 | tf_op jit(solution)/shard_map/slice | solution.py:33
where the time goes:
time: 157 us
  blocking collectives  98.1 us (62%)
  other arithmetic  32.9 us (21%)
  matrix products  23.7 us (15%)
  local copies, waits for them, and re-layouts  1.89 us (1%)
    all_to_all x1, blocking collectives, local(): lax.all_to_all(packed, 'row', split_axis=2, concat_axis=0, tiled=True)  98.1 us
    dot_general x1, other arithmetic, local(): jnp.einsum('ts,tcfr->fcsr', source_hot, weighted, preferred_element_type=...  14.4 us
    dot_general x1, matrix products, local(): jnp.einsum('ts,tcfr->fcsr', source_hot, weighted, preferred_element_type=...  13.1 us
    another operation x3, other arithmetic  10 us
    dot_general x1, matrix products, local(): jnp.einsum('ts,tr->sr', source_hot, receiver_hot, preferred_element_type=...  7.13 us
    convert_element_type x1, other arithmetic, local(): (receiver_value[:, None] == receiver_range[None, :]).astype(jnp.bfloat16)  4.92 us
    dot_general x1, matrix products, local(): jnp.dot(shot_traces, table, preferred_element_type=jnp.float32)  3.49 us

commit v1 on v0

v1 whole, which is shorter than its diff:
```python
import functools
import math

import jax
import jax.numpy as jnp
import numpy as np
from jax import lax
from jax.experimental import pallas as pl
from jax.experimental.pallas import tpu as pltpu
from jax.sharding import PartitionSpec as P

FLO = 64
SC = 128
RC = 128
MESH = pl.DeviceIdType.MESH
NT_DIMS = (((1,), (1,)), ((), ()))
CHUNKS = 4
STRIDE = 4
SELF = 31
FAR = 30


def twiddles(samples, band):
    bins = FLO + np.arange(band, dtype=np.int64)
    phase = (np.arange(samples, dtype=np.int64)[:, None] * bins[None, :]) % samples
    angle = (2.0 * math.pi * phase.astype(np.float32) / samples).astype(np.float32)
    scale = 1.0 / math.sqrt(samples)
    table = np.concatenate([np.cos(angle) * scale, -np.sin(angle) * scale], axis=1)
    return jnp.asarray(table.astype(np.float32)).astype(jnp.bfloat16)


def final_base(level, side):
    return 24 + 4 * (2 * (level - 1) + side)


def transit_base(level, hop, side):
    if hop == level:
        return final_base(level, side)
    return 48 + 4 * (2 * {(2, 1): 0, (3, 1): 1, (3, 2): 2}[(level, hop)] + side)


FAR_BASE = 72
SLOTS = 76


def leg_cell(level, side):
    return 24 + 2 * (level - 1) + side


def kernel(
    chips,
    traces_hbm,
    table_hbm,
    source_ref,
    receiver_ref,
    order_ref,
    stack_ref,
    counts_ref,
    traces,
    table,
    acc,
    staged,
    own,
    give,
    slots,
    cells,
    total,
    load_sem,
    send_sem,
    recv_sem,
):
    me = lax.axis_index("row")
    z = me // 2
    core = me % 2
    band = order_ref.shape[1]
    samples = traces.shape[1]
    part = samples // CHUNKS

    def peer(step):
        return {"row": ((z + step + chips) % chips) * 2 + core}

    partner = {"row": z * 2 + (1 - core)}
    towards = (1, -1)
    far_way = 1 - 2 * core

    loads = []
    for k in range(CHUNKS):
        span = pl.ds(k * part, part)
        loads.append(
            (
                pltpu.make_async_copy(table_hbm.at[span, :], table.at[span, :], load_sem.at[2 * k]),
                pltpu.make_async_copy(
                    traces_hbm.at[:, span], traces.at[:, span], load_sem.at[2 * k + 1]
                ),
            )
        )
    for pair in loads:
        for copy in pair:
            copy.start()

    barrier = pltpu.get_barrier_semaphore()
    greeted = [partner] + [peer(way * step) for step in range(1, STRIDE + 1) for way in towards]
    for who in greeted:
        pl.semaphore_signal(barrier, inc=1, device_id=who, device_id_type=MESH)

    source = source_ref[...]
    cells[SELF, 0, 0:4, :] = (source // 2).astype(jnp.float32).astype(jnp.bfloat16)
    cells[SELF, 0, 4:8, :] = (
        ((source % 2) * RC + receiver_ref[...]).astype(jnp.float32).astype(jnp.bfloat16)
    )
    total[...] = jnp.zeros_like(total)

    row = lax.broadcasted_iota(jnp.int32, (band, band), 0)
    col = lax.broadcasted_iota(jnp.int32, (band, band), 1)
    wanted = 4 * ((z + row % 32) % chips) + 2 * ((core + (row // 32) % 2) % 2) + row // 64
    place = (wanted == col).astype(jnp.float32).astype(jnp.bfloat16)
    holds = (row == jnp.broadcast_to(order_ref[...], (band, band))).astype(jnp.float32)
    pick = lax.dot_general(
        place, holds.astype(jnp.bfloat16), NT_DIMS, preferred_element_type=jnp.float32
    ).astype(jnp.bfloat16)

    for k in range(CHUNKS):
        span = pl.ds(k * part, part)
        for copy in loads[k]:
            copy.wait()
        piece = jnp.dot(traces[:, span], table[span, :], preferred_element_type=jnp.float32)
        if k == 0:
            acc[...] = piece
        else:
            acc[...] += piece
    for c in range(2):
        half = acc[:, c * band : (c + 1) * band].astype(jnp.bfloat16)
        turned = lax.dot_general(pick, half, NT_DIMS, preferred_element_type=jnp.float32)
        for f in range(2):
            for x in range(2):
                for b in range(4):
                    staged[pl.ds(x * 512 + b * 4 + c * 2 + f, 32, stride=16), :] = turned[
                        f * 64 + x * 32 : f * 64 + x * 32 + 32, b * 128 : (b + 1) * 128
                    ]
    own[:, 0, :, :] = staged[0:512, :].reshape(32, 16, 128).astype(jnp.bfloat16)
    give[...] = staged[512:1024, :].reshape(32, 16, 128).astype(jnp.bfloat16)

    pl.semaphore_wait(barrier, len(greeted))

    started = []

    def send(src, dst, who):
        n = len(started)
        copy = pltpu.make_async_remote_copy(
            src_ref=src,
            dst_ref=dst,
            send_sem=send_sem.at[n],
            recv_sem=recv_sem.at[n],
            device_id=who,
            device_id_type=MESH,
        )
        copy.start()
        started.append(copy)
        return copy

    def swap_cells(first, count):
        return send(cells.at[pl.ds(first, count), 0], cells.at[pl.ds(first, count), 1], partner)

    def send_cells(src, level):
        out = []
        for step in range(1, 4):
            for side in range(2):
                out.append(
                    send(
                        cells.at[src[side], 0],
                        cells.at[6 * level + 3 * side + step - 1, 0],
                        peer(towards[side] * step),
                    )
                )
        return out

    leg = {}
    near_cells = {}
    swaps = {}
    leg[1] = [send(cells.at[SELF, 0], cells.at[leg_cell(1, s), 0], peer(4 * towards[s])) for s in range(2)]
    swaps["self"] = swap_cells(SELF, 1)
    swap_data = send(give, own.at[:, 1], partner)

    def sources(level, side):
        return 4 * level if side == 0 else 32 - 4 * level - 3

    hops = {}
    for lane in range(2):
        if lane == 1:
            swap_data.wait_recv()
        hops["far", 1, lane] = send(own.at[16, lane], slots.at[FAR_BASE, lane], peer(4 * far_way))
        for s in range(2):
            base = transit_base(3, 1, s)
            hops[3, 1, s, lane] = send(
                own.at[pl.ds(sources(3, s), 4), lane],
                slots.at[pl.ds(base, 4), lane],
                peer(4 * towards[s]),
            )
    near_cells[0] = send_cells((SELF, SELF), 0)
    for level in (2, 1):
        for s in range(2):
            base = transit_base(level, 1, s)
            hops[level, 1, s] = send(
                own.at[pl.ds(sources(level, s), 4)], slots.at[pl.ds(base, 4)], peer(4 * towards[s])
            )
    near = {0: []}
    for step in range(1, 4):
        for s in range(2):
            index = step if s == 0 else 32 - step
            near[0].append(
                send(own.at[index], slots.at[3 * s + step - 1], peer(towards[s] * step))
            )

    line = lax.broadcasted_iota(jnp.int32, (16, 128), 0).astype(jnp.float32)
    lines = [(line + 16.0 * g).astype(jnp.bfloat16) for g in range(16)]
    one = jnp.ones((16, 128), jnp.bfloat16)
    none = jnp.zeros((16, 128), jnp.bfloat16)

    def spread(rows, n):
        return jnp.broadcast_to(rows[n : n + 1, :], (16, 128)).astype(jnp.bfloat16)

    def binned(block, at, where):
        result = None
        for lane in range(2):
            value = block[at, lane].astype(jnp.float32)
            cell = cells[where, lane].astype(jnp.float32)
            for pair in range(2):
                left, right = [], []
                for b in (2 * pair, 2 * pair + 1):
                    high = spread(cell, b)
                    low = spread(cell, 4 + b)
                    hit = [high == lines[g] for g in range(4)]
                    rows = []
                    for cf in range(4):
                        v = spread(value, b * 4 + cf)
                        rows += [jnp.where(h, v, none) for h in hit]
                    rows += [jnp.where(h, one, none) for h in hit]
                    left.append(jnp.concatenate(rows, axis=0))
                    right.append(
                        jnp.concatenate([jnp.where(low == g, one, none) for g in lines], axis=0)
                    )
                piece = lax.dot_general(
                    jnp.concatenate(left, axis=1),
                    jnp.concatenate(right, axis=1),
                    NT_DIMS,
                    preferred_element_type=jnp.float32,
                )
                result = piece if result is None else result + piece
        total[...] += result

    def bin_many(first, pace, count, cell):
        def body(n, carry):
            binned(slots, first + pace * n, cell + n)
            return carry

        lax.fori_loop(0, count, body, 0)

    def wait_all(copies):
        for copy in copies:
            copy.wait_recv()

    def cells_step(level):
        wait_all(leg[level])
        if level < 3:
            leg[level + 1] = [
                send(cells.at[leg_cell(level, s), 0], cells.at[leg_cell(level + 1, s), 0], peer(4 * towards[s]))
                for s in range(2)
            ]
        else:
            leg[4] = [send(cells.at[leg_cell(3, 0) + core, 0], cells.at[FAR, 0], peer(4 * far_way))]
        near_cells[level] = send_cells((leg_cell(level, 0), leg_cell(level, 1)), level)
        swaps["leg", level] = swap_cells(leg_cell(level, 0), 2)

    def near_swap(level):
        wait_all(near_cells[level])
        swaps["near", level] = swap_cells(6 * level, 6)

    def onward(level, hop):
        for s in range(2):
            hops[level, hop, s].wait_recv()
            hops[level, hop + 1, s] = send(
                slots.at[pl.ds(transit_base(level, hop, s), 4)],
                slots.at[pl.ds(transit_base(level, hop + 1, s), 4)],
                peer(4 * towards[s]),
            )

    def far_onward(hop):
        if hop > 1:
            hops["far", hop].wait_recv()
        hops["far", hop + 1] = send(
            slots.at[FAR_BASE + hop - 1], slots.at[FAR_BASE + hop], peer(4 * far_way)
        )

    def deliver(level):
        for s in range(2):
            hops[level, level, s].wait_recv()
        near[level] = []
        for step in (3, 2, 1):
            for s in range(2):
                base = final_base(level, s)
                near[level].append(
                    send(
                        slots.at[base + (step if s == 0 else 3 - step)],
                        slots.at[6 * level + 3 * s + step - 1],
                        peer(towards[s] * step),
                    )
                )

    def bin_legs(level):
        swaps["leg", level].wait_recv()
        bin_many(final_base(level, 0), 7, 2, leg_cell(level, 0))

    def bin_near(level):
        wait_all(near[level])
        swaps["near", level].wait_recv()
        bin_many(6 * level, 1, 6, 6 * level)

    swaps["self"].wait_recv()
    binned(own, 0, SELF)
    cells_step(1)
    for lane in range(2):
        hops["far", 1, lane].wait_recv()
    far_onward(1)
    for s in range(2):
        hops[3, 1, s, 0].wait_recv()
        hops[3, 1, s] = hops[3, 1, s, 1]
    onward(3, 1)
    near_swap(0)
    onward(2, 1)
    cells_step(2)
    bin_near(0)
    near_swap(1)
    deliver(1)
    bin_legs(1)
    far_onward(2)
    onward(3, 2)
    cells_step(3)
    bin_near(1)
    near_swap(2)
    deliver(2)
    bin_legs(2)
    far_onward(3)
    wait_all(leg[4])
    swaps["far"] = swap_cells(FAR, 1)
    near_swap(3)
    bin_near(2)
    deliver(3)
    bin_legs(3)
    hops["far", 4].wait_recv()
    swaps["far"].wait_recv()
    bin_many(FAR_BASE + 3, 1, 1, FAR)
    bin_near(3)

    for cf in range(4):
        for odd in range(2):
            stack_ref[cf % 2, cf // 2, pl.ds(odd, 64, stride=2), :] = total[
                cf * 64 : cf * 64 + 64, odd * 128 : odd * 128 + 128
            ]
    for odd in range(2):
        counts_ref[pl.ds(odd, 64, stride=2), :] = total[256:320, odd * 128 : odd * 128 + 128]
    for copy in started:
        copy.wait_send()


COPIES = 100


def solution(mesh):
    rows = mesh.shape["row"]

    def local(shot_traces, source_cell, receiver_cell, band_order):
        count, samples = shot_traces.shape
        band = band_order.shape[0]
        per = band // rows
        vmem = pl.BlockSpec(memory_space=pltpu.VMEM)
        anywhere = pl.BlockSpec(memory_space=pl.ANY)
        stack, counts = pl.pallas_call(
            functools.partial(kernel, rows // 2),
            out_shape=(
                jax.ShapeDtypeStruct((per, 2, SC, RC), jnp.float32),
                jax.ShapeDtypeStruct((SC, RC), jnp.float32),
            ),
            in_specs=[anywhere, anywhere, vmem, vmem, vmem],
            out_specs=(vmem, vmem),
            scratch_shapes=[
                pltpu.VMEM((count, samples), jnp.bfloat16),
                pltpu.VMEM((samples, 2 * band), jnp.bfloat16),
                pltpu.VMEM((count, 2 * band), jnp.float32),
                pltpu.VMEM((1024, 128), jnp.float32),
                pltpu.VMEM((32, 2, 16, 128), jnp.bfloat16),
                pltpu.VMEM((32, 16, 128), jnp.bfloat16),
                pltpu.VMEM((SLOTS, 2, 16, 128), jnp.bfloat16),
                pltpu.VMEM((32, 2, 8, 128), jnp.bfloat16),
                pltpu.VMEM((320, 256), jnp.float32),
                pltpu.SemaphoreType.DMA((2 * CHUNKS,)),
                pltpu.SemaphoreType.DMA((COPIES,)),
                pltpu.SemaphoreType.DMA((COPIES,)),
            ],
            compiler_params=pltpu.CompilerParams(collective_id=0, has_side_effects=True),
        )(
            shot_traces,
            twiddles(samples, band),
            source_cell.reshape(4, 128),
            receiver_cell.reshape(4, 128),
            band_order.reshape(1, band),
        )
        return stack / jnp.maximum(counts, 1.0)[None, None, :, :]

    placed = (P(("band", "row"), None), P(("band", "row")), P(("band", "row")), P("band"))
    return jax.shard_map(
        local,
        mesh=mesh,
        in_specs=placed,
        out_specs=P(("band", "row"), None, None, None),
        check_vma=False,
    )
```

time: 157 us -> 69.7 us (0.44)
  blocking collectives: 98.1 us -> 0 us
  Pallas kernels: 0 us -> 67 us
  other arithmetic: 32.9 us -> 2.52 us
  matrix products: 23.7 us -> 0 us
  local copies, waits for them, and re-layouts: 1.89 us -> 0 us
    all_to_all x1 -> x0, blocking collectives: 98.1 us -> none  [local(): lax.all_to_all(packed, 'row', split_axis=2, concat_axis=0, tiled=True)]
    pallas_call x0 -> x1, Pallas kernels: none -> 67 us  [local(): pl.pallas_call(functools.partial(kernel, rows // 2), out_shape=(jax.Shape...]
    dot_general x3 -> x0, matrix products: 23.7 us -> none  [the longest x1 13.1 us: local(): jnp.einsum('ts,tcfr->fcsr', source_hot, weighted, preferred_element_type=...]
    dot_general x2 -> x0, other arithmetic: 16.6 us -> none  [the longest x1 14.4 us: local(): jnp.einsum('ts,tcfr->fcsr', source_hot, weighted, preferred_element_type=...]
    another operation x4 -> x0, other arithmetic: 10 us -> none
    convert_element_type x2 -> x0, other arithmetic: 5.1 us -> none  [the longest x1 4.92 us: local(): (receiver_value[:, None] == receiver_range[None, :]).astype(jnp.bfloat16)]
    div x0 -> x1, other arithmetic: none -> 1.68 us  [local(): return stack / jnp.maximum(counts, 1.0)[None, None, :, :]]
where the time goes in v1:
time: 69.7 us; the launch traced here: 69.5 us
  Pallas kernels  67 us (96%)
  other arithmetic  2.52 us (4%)
    pallas_call x1, Pallas kernels, local(): pl.pallas_call(functools.partial(kernel, rows // 2), out_shape=(jax.Shape...  67 us
    div x1, other arithmetic, local(): return stack / jnp.maximum(counts, 1.0)[None, None, :, :]  1.68 us

profile of v1, /device:TPU:37, one launch (start us, length us, event | category | flops | bytes accessed | tf_op | source)
XLA Modules:
  0.0 69.5 jit_solution(9918515721304605890)
XLA Ops:
  0.0 67.0 %shard_map.55 = (f32[2,2,128,128]{3,2,1,0:T(8,128)}, f32[128,128]{1,0:T(8,128)}) custom-call(bf16[512,4096]{1,0:T(8,128)(2,1)} %traces_hbm.1, bf16[4096,256]{1,0:T(8,128)(2,1)} %constant.5.table_hbm, s32[4,128]{1,0:T(4,128)} %bitcast.3, s32[4,128]{1,0:T(4,128)} %bitcast.4, s32[1,128]{1,0:T(1,128)} %bitcast.5), custom_call_target="tpu_custom_call" | custom-call | tf_op jit(solution)/shard_map/pallas_call | solution.py:377
  67.0 0.8 %broadcast_maximum_fusion = f32[128,128]{1,0:T(8,128)S(1)} fusion(f32[128,128]{1,0:T(8,128)} %get-tuple-element.8), kind=kLoop, calls=%fused_computation.1 | loop fusion | flops 16384 | bytes 131072 | tf_op jit(solution)/shard_map/max | solution.py:407
  67.8 1.7 %broadcast_divide_fusion = f32[2,2,128,128]{3,2,1,0:T(8,128)} fusion(f32[2,2,128,128]{3,2,1,0:T(8,128)} %get-tuple-element.7, f32[128,128]{1,0:T(8,128)S(1)} %broadcast_maximum_fusion), kind=kLoop, calls=%fused_computation | loop fusion | flops 65536 | bytes 589824 | tf_op jit(solution)/shard_map/div | solution.py:407

commit v2 on v0

v2 whole, which is shorter than its diff:
```python
import functools
import math

import jax
import jax.numpy as jnp
import numpy as np
from jax import lax
from jax.experimental import pallas as pl
from jax.experimental.pallas import tpu as pltpu
from jax.sharding import PartitionSpec as P

FLO = 64
SC = 128
RC = 128
MESH = pl.DeviceIdType.MESH
NT_DIMS = (((1,), (1,)), ((), ()))
CHUNKS = 4
REACH = 8


def twiddles(samples, band):
    bins = FLO + np.arange(band, dtype=np.int64)
    phase = (np.arange(samples, dtype=np.int64)[:, None] * bins[None, :]) % samples
    angle = (2.0 * math.pi * phase.astype(np.float32) / samples).astype(np.float32)
    scale = 1.0 / math.sqrt(samples)
    table = np.concatenate([np.cos(angle) * scale, -np.sin(angle) * scale], axis=1)
    return jnp.asarray(table.astype(np.float32)).astype(jnp.bfloat16)


FAR = 30
SELF = 31
TRANSIT = 32
SLOTS = TRANSIT + 16
FAR_TRANSIT = TRANSIT + 7
CHUNKED = ((14, 15), (12, 13), (10, 11), (9, 9))


def place_of(distance, side):
    return 2 * (distance - 1) + side


def transit_of(chunk, side):
    first, last = CHUNKED[chunk]
    return TRANSIT + 8 * side + (first - 9 if side == 0 else 15 - last)


def sources_of(chunk, side):
    first, last = CHUNKED[chunk]
    return first if side == 0 else 32 - last


ORDER = (
    ("chunk", 0),
    ("spread", 0),
    ("direct", 1),
    ("direct", 2),
    ("direct", 3),
    ("cells", 4),
    ("chunk", 1),
    ("direct", 8),
    ("cells", 8),
    ("chunk", 2),
    ("swap", 0),
    ("direct", 7),
    ("chunk", 3),
    ("swap", 4),
    ("bin", 1, 3),
    ("relay", 0),
    ("cells", 12),
    ("direct", 6),
    ("swap", 8),
    ("relay", 1),
    ("direct", 5),
    ("direct", 4),
    ("bin", 8, 8),
    ("swap", 12),
    ("relay", 2),
    ("bin", 7, 7),
    ("relay", 3),
    ("bin", 15, 16),
    ("bin", 13, 14),
    ("bin", 6, 6),
    ("bin", 11, 12),
    ("bin", 9, 10),
    ("bin", 4, 5),
)


def kernel(
    chips,
    traces_hbm,
    table_hbm,
    source_ref,
    receiver_ref,
    order_ref,
    stack_ref,
    counts_ref,
    traces,
    table,
    acc,
    staged,
    own,
    slots,
    cells,
    total,
    load_sem,
    send_sem,
    recv_sem,
):
    me = lax.axis_index("row")
    z = me // 2
    core = me % 2
    band = order_ref.shape[1]
    samples = traces.shape[1]
    part = samples // CHUNKS

    def peer(step, cross=0):
        return {"row": ((z + step + chips) % chips) * 2 + (core + cross) % 2}

    partner = peer(0, 1)
    towards = (1, -1)
    far_way = 1 - 2 * core

    loads = []
    for k in range(CHUNKS):
        span = pl.ds(k * part, part)
        loads.append(
            (
                pltpu.make_async_copy(table_hbm.at[span, :], table.at[span, :], load_sem.at[2 * k]),
                pltpu.make_async_copy(
                    traces_hbm.at[:, span], traces.at[:, span], load_sem.at[2 * k + 1]
                ),
            )
        )
    for pair in loads:
        for copy in pair:
            copy.start()

    barrier = pltpu.get_barrier_semaphore()
    greeted = [partner] + [
        peer(way * step, cross)
        for step in range(1, REACH + 1)
        for way in towards
        for cross in range(2)
    ]
    for who in greeted:
        pl.semaphore_signal(barrier, inc=1, device_id=who, device_id_type=MESH)

    source = source_ref[...]
    cells[SELF, 0, 0:4, :] = (source // 2).astype(jnp.float32).astype(jnp.bfloat16)
    cells[SELF, 0, 4:8, :] = (
        ((source % 2) * RC + receiver_ref[...]).astype(jnp.float32).astype(jnp.bfloat16)
    )
    total[...] = jnp.zeros_like(total)

    row = lax.broadcasted_iota(jnp.int32, (band, band), 0)
    col = lax.broadcasted_iota(jnp.int32, (band, band), 1)
    wanted = 4 * ((z + row % 32) % chips) + 2 * ((core + (row // 32) % 2) % 2) + row // 64
    place = (wanted == col).astype(jnp.float32).astype(jnp.bfloat16)
    holds = (row == jnp.broadcast_to(order_ref[...], (band, band))).astype(jnp.float32)
    pick = lax.dot_general(
        place, holds.astype(jnp.bfloat16), NT_DIMS, preferred_element_type=jnp.float32
    ).astype(jnp.bfloat16)

    for k in range(CHUNKS):
        span = pl.ds(k * part, part)
        for copy in loads[k]:
            copy.wait()
        piece = jnp.dot(traces[:, span], table[span, :], preferred_element_type=jnp.float32)
        if k == 0:
            acc[...] = piece
        else:
            acc[...] += piece
    for c in range(2):
        half = acc[:, c * band : (c + 1) * band].astype(jnp.bfloat16)
        turned = lax.dot_general(pick, half, NT_DIMS, preferred_element_type=jnp.float32)
        for f in range(2):
            for x in range(2):
                for b in range(4):
                    staged[pl.ds(x * 16 + b * 4 + c * 2 + f, 32, stride=32), :] = turned[
                        f * 64 + x * 32 : f * 64 + x * 32 + 32, b * 128 : (b + 1) * 128
                    ]
    own[...] = staged[...].reshape(32, 2, 16, 128).astype(jnp.bfloat16)
    slots[SELF, 0] = own[0, 0]

    pl.semaphore_wait(barrier, len(greeted))

    started = []

    def send(src, dst, who):
        n = len(started)
        copy = pltpu.make_async_remote_copy(
            src_ref=src,
            dst_ref=dst,
            send_sem=send_sem.at[n],
            recv_sem=recv_sem.at[n],
            device_id=who,
            device_id_type=MESH,
        )
        copy.start()
        started.append(copy)
        return copy

    def swap_cells(first, count):
        return send(cells.at[pl.ds(first, count), 0], cells.at[pl.ds(first, count), 1], partner)

    legs, spreads, swaps, arrivals, transits = {}, {}, {}, {}, {}

    def wait_all(copies):
        for copy in copies:
            copy.wait_recv()

    def cells_leg(distance, froms, hop):
        legs[distance] = [
            send(cells.at[froms[s], 0], cells.at[place_of(distance, s), 0], peer(hop * towards[s]))
            for s in range(2)
        ]

    def spread_cells(base):
        froms = (place_of(base, 0), place_of(base, 1)) if base else (SELF, SELF)
        spreads[base] = [
            send(
                cells.at[froms[s], 0],
                cells.at[place_of(base + step, s), 0],
                peer(towards[s] * step),
            )
            for step in (3, 2, 1)
            for s in range(2)
        ]

    def cells_onward(base):
        wait_all(legs[base])
        here = (place_of(base, 0), place_of(base, 1))
        if base == 8:
            cells_leg(12, here, 4)
            legs[16] = [send(cells.at[here[0] + core, 0], cells.at[FAR, 0], peer(8 * far_way))]
        spread_cells(base)
        swaps[base] = swap_cells(here[0], 2)

    def near_swap(base):
        wait_all(spreads[base])
        swap = swap_cells(place_of(base + 1, 0), 6)
        for step in (1, 2, 3):
            swaps[base + step] = swap
        if base == 12:
            wait_all(legs[16])
            swaps[16] = swap_cells(FAR, 1)

    def chunk(k):
        first, last = CHUNKED[k]
        size = last - first + 1
        if k == 0:
            transits["far"] = [send(own.at[16], slots.at[FAR_TRANSIT], peer(REACH * far_way))]
        transits[k] = [
            send(
                own.at[pl.ds(sources_of(k, s), size)],
                slots.at[pl.ds(transit_of(k, s), size)],
                peer(REACH * towards[s]),
            )
            for s in range(2)
        ]

    def direct(step):
        arrivals[step] = [
            send(
                own.at[step if s == 0 else 32 - step, cross],
                slots.at[place_of(step, s), cross],
                peer(towards[s] * step, cross),
            )
            for s in range(2)
            for cross in range(2)
        ]

    def relay(k):
        if k == 0:
            wait_all(transits["far"])
            arrivals[16] = [arrived_self] + [
                send(slots.at[FAR_TRANSIT, x], slots.at[FAR, x], peer(REACH * far_way, x))
                for x in range(2)
            ]
        wait_all(transits[k])
        first, last = CHUNKED[k]
        for distance in range(last, first - 1, -1):
            arrivals[distance] = [
                send(
                    slots.at[TRANSIT + 8 * s + (distance - 9 if s == 0 else 15 - distance), cross],
                    slots.at[place_of(distance, s), cross],
                    peer(towards[s] * (distance - REACH), cross),
                )
                for s in range(2)
                for cross in range(2)
            ]

    cells_leg(8, (SELF, SELF), 8)
    cells_leg(4, (SELF, SELF), 4)
    swap_self = swap_cells(SELF, 1)
    arrived_self = send(own.at[0, 1], slots.at[SELF, 1], partner)

    line = lax.broadcasted_iota(jnp.int32, (16, 128), 0).astype(jnp.float32)
    lines = [(line + 16.0 * g).astype(jnp.bfloat16) for g in range(4)]
    lane = lax.broadcasted_iota(jnp.int32, (16, 128), 1).astype(jnp.float32)
    lanes = [
        jnp.concatenate([(lane + 128.0 * g).astype(jnp.bfloat16)] * 8, axis=0) for g in range(2)
    ]
    one = jnp.ones((16, 128), jnp.bfloat16)
    none = jnp.zeros((16, 128), jnp.bfloat16)
    ones = jnp.ones((128, 128), jnp.bfloat16)
    nones = jnp.zeros((128, 128), jnp.bfloat16)

    def spread(rows, n, size=16):
        return jnp.broadcast_to(rows[n : n + 1, :], (size, 128)).astype(jnp.bfloat16)

    def binned(first, last):
        result = None
        for at in range(2 * first, 2 * last + 2):
            for cross in range(2):
                value = slots[at, cross].astype(jnp.float32)
                cell = cells[at, cross].astype(jnp.float32)
                for pair in range(2):
                    left, right = [], []
                    for b in (2 * pair, 2 * pair + 1):
                        high = spread(cell, b)
                        hit = [high == lines[g] for g in range(4)]
                        rows = []
                        for cf in range(4):
                            v = spread(value, b * 4 + cf)
                            rows += [jnp.where(h, v, none) for h in hit]
                        rows += [jnp.where(h, one, none) for h in hit]
                        left.append(jnp.concatenate(rows, axis=0))
                        low = spread(cell, 4 + b, 128).T
                        right.append(
                            jnp.concatenate(
                                [jnp.where(low == g, ones, nones) for g in lanes], axis=1
                            )
                        )
                    piece = jnp.dot(
                        jnp.concatenate(left, axis=1),
                        jnp.concatenate(right, axis=0),
                        preferred_element_type=jnp.float32,
                    )
                    result = piece if result is None else result + piece
        total[...] += result

    waited = []

    def bin_span(first, last):
        for distance in range(first, last + 1):
            wait_all(arrivals[distance])
            for swap in (swaps[distance], swap_self) if distance == 16 else (swaps[distance],):
                if not any(swap is other for other in waited):
                    waited.append(swap)
                    swap.wait_recv()
        binned(first - 1, last - 1)

    steps = {
        "chunk": chunk,
        "direct": direct,
        "relay": relay,
        "spread": spread_cells,
        "cells": cells_onward,
        "swap": near_swap,
        "bin": bin_span,
    }
    for what, *given in ORDER:
        steps[what](*given)

    for cf in range(4):
        for odd in range(2):
            stack_ref[cf % 2, cf // 2, pl.ds(odd, 64, stride=2), :] = total[
                cf * 64 : cf * 64 + 64, odd * 128 : odd * 128 + 128
            ]
    for odd in range(2):
        counts_ref[pl.ds(odd, 64, stride=2), :] = jnp.maximum(
            total[256:320, odd * 128 : odd * 128 + 128], 1.0
        )
    for copy in started:
        copy.wait_send()


COPIES = 140


def solution(mesh):
    rows = mesh.shape["row"]

    def local(shot_traces, source_cell, receiver_cell, band_order):
        count, samples = shot_traces.shape
        band = band_order.shape[0]
        per = band // rows
        vmem = pl.BlockSpec(memory_space=pltpu.VMEM)
        anywhere = pl.BlockSpec(memory_space=pltpu.HBM)
        stack, counts = pl.pallas_call(
            functools.partial(kernel, rows // 2),
            out_shape=(
                jax.ShapeDtypeStruct((per, 2, SC, RC), jnp.float32),
                jax.ShapeDtypeStruct((SC, RC), jnp.float32),
            ),
            in_specs=[anywhere, anywhere, vmem, vmem, vmem],
            out_specs=(vmem, vmem),
            scratch_shapes=[
                pltpu.VMEM((count, samples), jnp.bfloat16),
                pltpu.VMEM((samples, 2 * band), jnp.bfloat16),
                pltpu.VMEM((count, 2 * band), jnp.float32),
                pltpu.VMEM((1024, 128), jnp.float32),
                pltpu.VMEM((32, 2, 16, 128), jnp.bfloat16),
                pltpu.VMEM((SLOTS, 2, 16, 128), jnp.bfloat16),
                pltpu.VMEM((32, 2, 8, 128), jnp.bfloat16),
                pltpu.VMEM((320, 256), jnp.float32),
                pltpu.SemaphoreType.DMA((2 * CHUNKS,)),
                pltpu.SemaphoreType.DMA((COPIES,)),
                pltpu.SemaphoreType.DMA((COPIES,)),
            ],
            compiler_params=pltpu.CompilerParams(
                collective_id=0, has_side_effects=True, vmem_limit_bytes=55_000_000
            ),
        )(
            shot_traces,
            twiddles(samples, band),
            source_cell.reshape(4, 128),
            receiver_cell.reshape(4, 128),
            band_order.reshape(1, band),
        )
        return stack / counts[None, None, :, :]

    placed = (P(("band", "row"), None), P(("band", "row")), P(("band", "row")), P("band"))
    return jax.shard_map(
        local,
        mesh=mesh,
        in_specs=placed,
        out_specs=P(("band", "row"), None, None, None),
        check_vma=False,
    )
```

time: 157 us -> 67.8 us (0.43)
  blocking collectives: 98.1 us -> 0 us
  Pallas kernels: 0 us -> 64.9 us
  other arithmetic: 32.9 us -> 0.73 us
  matrix products: 23.7 us -> 0 us
    all_to_all x1 -> x0, blocking collectives: 98.1 us -> none  [local(): lax.all_to_all(packed, 'row', split_axis=2, concat_axis=0, tiled=True)]
    pallas_call x0 -> x1, Pallas kernels: none -> 64.9 us  [local(): pl.pallas_call(functools.partial(kernel, rows // 2), out_shape=(jax.Shape...]
    dot_general x3 -> x0, matrix products: 23.7 us -> none  [the longest x1 13.1 us: local(): jnp.einsum('ts,tcfr->fcsr', source_hot, weighted, preferred_element_type=...]
    dot_general x2 -> x0, other arithmetic: 16.6 us -> none  [the longest x1 14.4 us: local(): jnp.einsum('ts,tcfr->fcsr', source_hot, weighted, preferred_element_type=...]
    another operation x4 -> x0, other arithmetic: 10 us -> none
    convert_element_type x2 -> x0, other arithmetic: 5.1 us -> none  [the longest x1 4.92 us: local(): (receiver_value[:, None] == receiver_range[None, :]).astype(jnp.bfloat16)]
    unnamed x2 -> x6, local copies, waits for them, and re-layouts: 0.01 us -> 2.02 us
where the time goes in v2:
time: 67.8 us; the launch traced here: 67.7 us
  Pallas kernels  64.9 us (96%)
  local copies, waits for them, and re-layouts  2.02 us (3%)
  other arithmetic  0.73 us (1%)
    pallas_call x1, Pallas kernels, local(): pl.pallas_call(functools.partial(kernel, rows // 2), out_shape=(jax.Shape...  64.9 us
    unnamed x6, local copies, waits for them, and re-layouts  2.02 us

profile of v2, /device:TPU:37, one launch (start us, length us, event | category | flops | bytes accessed | tf_op | source)
XLA Modules:
  0.0 67.7 jit_solution(16643531335919886938)
XLA Ops:
  0.0 0.0 copy-start
  0.0 0.7 %copy-done = s32[512]{0:T(512)S(1)} copy-done((s32[512]{0:T(512)S(1)}, s32[512]{0:T(512)}, u32[]{:S(2)}) %copy-start) | copy-done | bytes 2072
  0.7 0.0 copy-start.1
  0.7 0.7 %copy-done.1 = s32[512]{0:T(512)S(1)} copy-done((s32[512]{0:T(512)S(1)}, s32[512]{0:T(512)}, u32[]{:S(2)}) %copy-start.1) | copy-done | bytes 2072
  1.4 0.0 copy-start.2
  1.4 0.7 copy-done.2
  2.0 64.9 %shard_map.55 = (f32[2,2,128,128]{3,2,1,0:T(8,128)S(1)}, f32[128,128]{1,0:T(8,128)S(1)}) custom-call(bf16[512,4096]{1,0:T(8,128)(2,1)} %traces_hbm.1, bf16[4096,256]{1,0:T(8,128)(2,1)} %constant.3.table_hbm, s32[4,128]{1,0:T(4,128)S(1)} %bitcast.3, s32[4,128]{1,0:T(4,128)S(1)} %bitcast.4, s32[1,128]{1,0:T(1,128)S(1)} %bitcast.5), custom_call_target="tpu_custom_call" | custom-call | tf_op jit(solution)/shard_map/pallas_call | solution.py:392
  66.9 0.7 %broadcast_divide_fusion = f32[2,2,128,128]{3,2,1,0:T(8,128)} fusion(f32[2,2,128,128]{3,2,1,0:T(8,128)S(1)} %get-tuple-element.7, f32[128,128]{1,0:T(8,128)S(1)} %get-tuple-element.8), kind=kLoop, calls=%fused_computation | loop fusion | flops 65536 | bytes 589824 | tf_op jit(solution)/shard_map/div | solution.py:423
Async XLA Ops:
  0.0 0.7 %copy-start = (s32[512]{0:T(512)S(1)}, s32[512]{0:T(512)}, u32[]{:S(2)}) copy-start(s32[512]{0:T(512)} %param.6) | copy-start | bytes 6148
  0.7 0.7 %copy-start.1 = (s32[512]{0:T(512)S(1)}, s32[512]{0:T(512)}, u32[]{:S(2)}) copy-start(s32[512]{0:T(512)} %param.7) | copy-start | bytes 6148
  1.4 0.7 copy-start.2

commit v3 on v2

--- a/solution.py
+++ b/solution.py
@@ -90,13 +90,16 @@
     chips,
     traces_hbm,
     table_hbm,
-    source_ref,
-    receiver_ref,
-    order_ref,
+    source_hbm,
+    receiver_hbm,
+    order_hbm,
     stack_ref,
     counts_ref,
     traces,
     table,
+    source_ref,
+    receiver_ref,
+    order_ref,
     acc,
     staged,
     own,
@@ -121,6 +124,24 @@
     towards = (1, -1)
     far_way = 1 - 2 * core
 
+    barrier = pltpu.get_barrier_semaphore()
+    greeted = [partner] + [
+        peer(way * step, cross)
+        for step in range(REACH, 0, -1)
+        for way in towards
+        for cross in range(2)
+    ]
+    for who in greeted:
+        pl.semaphore_signal(barrier, inc=1, device_id=who, device_id_type=MESH)
+
+    small = [
+        pltpu.make_async_copy(src, dst, load_sem.at[2 * CHUNKS + n])
+        for n, (src, dst) in enumerate(
+            ((source_hbm, source_ref), (receiver_hbm, receiver_ref), (order_hbm, order_ref))
+        )
+    ]
+    for copy in small:
+        copy.start()
     loads = []
     for k in range(CHUNKS):
         span = pl.ds(k * part, part)
@@ -136,16 +157,8 @@
         for copy in pair:
             copy.start()
 
-    barrier = pltpu.get_barrier_semaphore()
-    greeted = [partner] + [
-        peer(way * step, cross)
-        for step in range(1, REACH + 1)
-        for way in towards
-        for cross in range(2)
-    ]
-    for who in greeted:
-        pl.semaphore_signal(barrier, inc=1, device_id=who, device_id_type=MESH)
-
+    for copy in small:
+        copy.wait()
     source = source_ref[...]
     cells[SELF, 0, 0:4, :] = (source // 2).astype(jnp.float32).astype(jnp.bfloat16)
     cells[SELF, 0, 4:8, :] = (
@@ -388,25 +401,28 @@
         band = band_order.shape[0]
         per = band // rows
         vmem = pl.BlockSpec(memory_space=pltpu.VMEM)
-        anywhere = pl.BlockSpec(memory_space=pltpu.HBM)
+        anywhere = pl.BlockSpec(memory_space=pl.ANY)
         stack, counts = pl.pallas_call(
             functools.partial(kernel, rows // 2),
             out_shape=(
                 jax.ShapeDtypeStruct((per, 2, SC, RC), jnp.float32),
                 jax.ShapeDtypeStruct((SC, RC), jnp.float32),
             ),
-            in_specs=[anywhere, anywhere, vmem, vmem, vmem],
+            in_specs=[anywhere] * 5,
             out_specs=(vmem, vmem),
             scratch_shapes=[
                 pltpu.VMEM((count, samples), jnp.bfloat16),
                 pltpu.VMEM((samples, 2 * band), jnp.bfloat16),
+                pltpu.VMEM((4, 128), jnp.int32),
+                pltpu.VMEM((4, 128), jnp.int32),
+                pltpu.VMEM((1, band), jnp.int32),
                 pltpu.VMEM((count, 2 * band), jnp.float32),
                 pltpu.VMEM((1024, 128), jnp.float32),
                 pltpu.VMEM((32, 2, 16, 128), jnp.bfloat16),
                 pltpu.VMEM((SLOTS, 2, 16, 128), jnp.bfloat16),
                 pltpu.VMEM((32, 2, 8, 128), jnp.bfloat16),
                 pltpu.VMEM((320, 256), jnp.float32),
-                pltpu.SemaphoreType.DMA((2 * CHUNKS,)),
+                pltpu.SemaphoreType.DMA((2 * CHUNKS + 3,)),
                 pltpu.SemaphoreType.DMA((COPIES,)),
                 pltpu.SemaphoreType.DMA((COPIES,)),
             ],
@@ -416,9 +432,9 @@
         )(
             shot_traces,
             twiddles(samples, band),
-            source_cell.reshape(4, 128),
-            receiver_cell.reshape(4, 128),
-            band_order.reshape(1, band),
+            pltpu.with_memory_space_constraint(source_cell.reshape(4, 128), pltpu.HBM),
+            pltpu.with_memory_space_constraint(receiver_cell.reshape(4, 128), pltpu.HBM),
+            pltpu.with_memory_space_constraint(band_order.reshape(1, band), pltpu.HBM),
         )
         return stack / counts[None, None, :, :]
 

time: 67.8 us -> 65.4 us (0.965)
  local copies, waits for them, and re-layouts: 2.02 us -> 0 us
    unnamed x6 -> x0, local copies, waits for them, and re-layouts: 2.02 us -> none
where the time goes in v3:
time: 65.4 us; the launch traced here: 65.3 us
  Pallas kernels  64.5 us (99%)
  other arithmetic  0.73 us (1%)
    pallas_call x1, Pallas kernels, local(): pl.pallas_call(functools.partial(kernel, rows // 2), out_shape=(jax.Shape...  64.5 us

profile of v3, /device:TPU:37, one launch (start us, length us, event | category | flops | bytes accessed | tf_op | source)
XLA Modules:
  0.0 65.3 jit_solution(822581105270033189)
XLA Ops:
  0.0 64.5 %shard_map.55 = (f32[2,2,128,128]{3,2,1,0:T(8,128)S(1)}, f32[128,128]{1,0:T(8,128)S(1)}) custom-call(bf16[512,4096]{1,0:T(8,128)(2,1)} %traces_hbm.1, bf16[4096,256]{1,0:T(8,128)(2,1)} %constant.3.table_hbm, s32[4,128]{1,0:T(4,128)} %bitcast.3, s32[4,128]{1,0:T(4,128)} %bitcast.4, s32[1,128]{1,0:T(1,128)} %bitcast.5), custom_call_target="tpu_custom_call" | custom-call | tf_op jit(solution)/shard_map/pallas_call | solution.py:405
  64.5 0.7 %broadcast_divide_fusion = f32[2,2,128,128]{3,2,1,0:T(8,128)} fusion(f32[2,2,128,128]{3,2,1,0:T(8,128)S(1)} %get-tuple-element.7, f32[128,128]{1,0:T(8,128)S(1)} %get-tuple-element.8), kind=kLoop, calls=%fused_computation | loop fusion | flops 65536 | bytes 589824 | tf_op jit(solution)/shard_map/div | solution.py:439
